TPU v7x, 8 devices: a whole 2x2x1 slice. The times are simulated.
8 devices in a mesh: data: 4 (over z, y, x), expert: 2 (over core).
Axes of the slice: x: 2, y: 2, z: 1, core: 2. Of those that a mesh axis runs over, the one named last changes fastest.
Arguments:
- dy: bfloat16 [32768, 768], P(('data', 'expert'))
- gates: float32 [32768, 1], P(('data', 'expert'))
- topk_idx: int32 [32768, 1], P(('data', 'expert'))
- slot: int32 [32768, 1], P(('data', 'expert'))
- yd: bfloat16 [32768, 1, 768], P(('data', 'expert'))
- xd: bfloat16 [32, 1280, 768], P(('data', 'expert'))
- h1: bfloat16 [32, 1280, 3072], P(('data', 'expert'))
- h3: bfloat16 [32, 1280, 3072], P(('data', 'expert'))
- w1: bfloat16 [8, 768, 3072], P('expert')
- w3: bfloat16 [8, 768, 3072], P('expert')
- w2: bfloat16 [8, 3072, 768], P('expert')
Outputs:
- output 1: bfloat16 [32768, 768], P(('data', 'expert'))
- output 2: float32 [32768, 1], P(('data', 'expert'))
- output 3: float32 [8, 768, 3072], P('expert', None, 'data')
- output 4: float32 [8, 768, 3072], P('expert', None, 'data')
- output 5: float32 [8, 3072, 768], P('expert', 'data')
All inputs are finite; a program needn't handle non-finite values.
Results may differ from a plain program's by a relative error of at most 0.0106909.
Values are sent between devices in bfloat16 or wider.
A program may use at most 1 GiB of HBM per device.

v0:
```python
import jax
import jax.numpy as jnp
from jax import lax
from jax.sharding import PartitionSpec as P

F32 = jnp.float32
BF16 = jnp.bfloat16


def _swiglu_bwd(dyd, xd, h1, h3, w1, w3, w2):
    h1f = h1.astype(F32)
    h3f = h3.astype(F32)
    s = jax.nn.sigmoid(h1f)
    silu = h1f * s
    a = (silu * h3f).astype(BF16)
    da = jnp.einsum('ecd,efd->ecf', dyd, w2, preferred_element_type=F32).astype(BF16).astype(F32)
    dh1 = (da * h3f * s * (1.0 + h1f * (1.0 - s))).astype(BF16)
    dh3 = (da * silu).astype(BF16)
    dxd = (jnp.einsum('ecf,edf->ecd', dh1, w1, preferred_element_type=F32)
           + jnp.einsum('ecf,edf->ecd', dh3, w3, preferred_element_type=F32)).astype(BF16)
    dw1 = jnp.einsum('ecd,ecf->edf', xd, dh1, preferred_element_type=F32)
    dw3 = jnp.einsum('ecd,ecf->edf', xd, dh3, preferred_element_type=F32)
    dw2 = jnp.einsum('ecf,ecd->efd', a, dyd, preferred_element_type=F32)
    return dxd, dw1, dw3, dw2


def solution(mesh):
    np_ = mesh.shape['expert']
    tok = P(('data', 'expert'), None)
    buf = P(('data', 'expert'), None, None)
    wsp = P('expert', None, None)

    def body(dy, gates, topk_idx, slot, yd, xd, h1, h3, w1, w3, w2):
        d = dy.shape[1]
        el = w1.shape[0]
        cap = xd.shape[1] // np_
        dg = jnp.einsum('tkd,td->tk', yd, dy, preferred_element_type=F32)
        v = (gates[:, :, None] * dy.astype(F32)[:, None, :]).astype(BF16)
        col = jnp.where(slot >= 0, slot, cap)
        send = jnp.zeros((np_ * el, cap, d), BF16).at[topk_idx, col].set(v, mode='drop')
        recv = lax.all_to_all(send.reshape(np_, el, cap, d), 'expert', 0, 0, tiled=True)
        dyd = jnp.swapaxes(recv, 0, 1).reshape(el, np_ * cap, d)
        dxd, dw1, dw3, dw2 = _swiglu_bwd(dyd, xd, h1, h3, w1, w3, w2)
        out = jnp.swapaxes(dxd.reshape(el, np_, cap, d), 0, 1)
        back = lax.all_to_all(out, 'expert', 0, 0, tiled=True).reshape(np_ * el, cap, d)
        got = back[topk_idx, jnp.minimum(col, cap - 1)].astype(F32)
        dx = jnp.sum(jnp.where((slot >= 0)[:, :, None], got, 0.0), axis=1).astype(BF16)
        dw1 = lax.psum_scatter(dw1, 'data', scatter_dimension=2, tiled=True)
        dw3 = lax.psum_scatter(dw3, 'data', scatter_dimension=2, tiled=True)
        dw2 = lax.psum_scatter(dw2, 'data', scatter_dimension=1, tiled=True)
        return dx, dg, dw1, dw3, dw2

    return jax.shard_map(body, mesh=mesh,
                         in_specs=(tok, tok, tok, tok, buf, buf, buf, buf, wsp, wsp, wsp),
                         out_specs=(tok, tok, P('expert', None, 'data'), P('expert', None, 'data'), P('expert', 'data', None)),
                         check_vma=False)
```

profile of v0, /device:TPU:0, one launch (start us, length us, event | category | flops | bytes accessed | tf_op | source)
XLA Modules:
  0.0 1113.6 jit_solution(16603949924139502848)
XLA Ops:
  7.2 0.0 reduce-scatter.4.cloned.1.call-start
  7.2 0.8 fusion.21
  8.0 0.8 and_reduce_fusion
  8.8 1.3 fusion.18
  10.1 24.2 %scatter_custom_fusion = bf16[5120,768]{1,0:T(8,128)(2,1)} fusion(s32[4096]{0:T(1024)S(1)} %broadcast_select_fusion, bf16[4096,768]{1,0:T(8,128)(2,1)} %param.11, f32[4096]{0:T(1024)} %bitcast.45, bf16[]{:T(256)} %constant.0.clone.1), kind=kCustom, calls=%fused_computation.29 | custom fusion | flops 9437184 | bytes 14172162
  34.3 12.4 %all_to_all.10 = bf16[2,4,640,768]{3,2,1,0:T(8,128)(2,1)S(1)} all-to-all(bf16[2,4,640,768]{3,2,1,0:T(8,128)(2,1)} %bitcast.37), channel_id=1, replica_groups=mesh['data'=4,'expert'=2] {'expert'}, dimensions={0} | all-to-all | bytes 15728640 | tf_op jit(solution)/shard_map/all_to_all | solution.py:41
  46.6 3.8 copy.29
  50.4 61.6 %fusion = (bf16[4,1280,3072]{2,1,0:T(8,128)(2,1)}, bf16[4,1280,3072]{2,1,0:T(8,128)(2,1)}) fusion(bf16[4,1280,3072]{2,1,0:T(8,128)(2,1)} %param.17, bf16[4,1280,3072]{2,1,0:T(8,128)(2,1)} %param.18, bf16[4,1280,768]{2,1,0:T(8,128)(2,1)} %bitcast.42, bf16[4,3072,768]{2,1,0:T(8,128)(2,1)} %param.21), kind=kOutput, calls=%fused_computation.8 | convolution fusion | flops 24426577920 | bytes 152567808 | tf_op jit(solution)/shard_map/ecd,efd->ecf/dot_general | solution.py:16
  112.0 35.3 %convolution_bitcast_fusion.1 = f32[4,768,3072]{1,2,0:T(8,128)} fusion(bf16[4,1280,3072]{2,1,0:T(8,128)(2,1)} %get-tuple-element.21, bf16[4,1280,768]{2,1,0:T(8,128)(2,1)} %param.16), kind=kOutput, calls=%fused_computation.23 | convolution fusion | flops 24159191040 | bytes 77070336 | tf_op jit(solution)/shard_map/ecd,ecf->edf/dot_general | solution.py:21
  147.3 0.0 reduce-scatter.4.cloned.1.call-update
  147.3 0.0 reduce-scatter.6.cloned.1.call-start
  147.4 35.3 %convolution_bitcast_fusion = f32[4,768,3072]{1,2,0:T(8,128)} fusion(bf16[4,1280,3072]{2,1,0:T(8,128)(2,1)} %get-tuple-element.20, bf16[4,1280,768]{2,1,0:T(8,128)(2,1)} %param.16), kind=kOutput, calls=%fused_computation.22 | convolution fusion | flops 24159191040 | bytes 77070336 | tf_op jit(solution)/shard_map/ecd,ecf->edf/dot_general | solution.py:22
  182.6 0.0 reduce-scatter.6.cloned.1.call-update
  182.7 0.0 reduce-scatter.8.cloned.1.call-start
  182.7 45.8 %fusion.9 = f32[4,3072,768]{2,1,0:T(8,128)} fusion(bf16[4,1280,768]{2,1,0:T(8,128)(2,1)} %bitcast.43, bf16[4,1280,3072]{2,1,0:T(8,128)(2,1)} %param.18, bf16[4,1280,3072]{2,1,0:T(8,128)(2,1)} %param.17), kind=kOutput, calls=%fused_computation.18 | convolution fusion | flops 24285020160 | bytes 108527616 | tf_op jit(solution)/shard_map/ecf,ecd->efd/dot_general | solution.py:23
  228.5 0.0 reduce-scatter.8.cloned.1.call-update
  228.5 31.8 %fusion.26 = f32[4,1280,768]{2,1,0:T(8,128)} fusion(bf16[4,1280,3072]{2,1,0:T(8,128)(2,1)} %get-tuple-element.21, bf16[4,768,3072]{2,1,0:T(8,128)(2,1)} %param.19), kind=kOutput, calls=%fused_computation.52 | convolution fusion | flops 24159191040 | bytes 66060288 | tf_op jit(solution)/shard_map/ecf,edf->ecd/dot_general | solution.py:19
  260.3 32.9 %add_convert_fusion = bf16[4,1280,768]{2,1,0:T(8,128)(2,1)} fusion(f32[4,1280,768]{2,1,0:T(8,128)} %fusion.26, bf16[4,1280,3072]{2,1,0:T(8,128)(2,1)} %get-tuple-element.20, bf16[4,768,3072]{2,1,0:T(8,128)(2,1)} %param.20), kind=kOutput, calls=%fused_computation.19 | convolution fusion | flops 24167055360 | bytes 73924608 | tf_op jit(solution)/shard_map/ecf,edf->ecd/dot_general | solution.py:20
  293.2 0.0 copy-start
  293.2 7.0 copy.45
  300.2 6.8 all-to-all-start.1
  306.9 0.0 copy-done
  306.9 0.1 fusion.23
  307.0 6.6 all-to-all-done.1
  313.6 0.0 copy-start.1
  313.6 114.9 %gather_fusion = bf16[4096,768]{1,0:T(8,128)(2,1)} fusion(bf16[8,640,768]{2,1,0:T(8,128)(2,1)} %bitcast.8, s32[4096]{0:T(1024)S(1)} %bitcast.36), kind=kCustom, calls=%fused_computation | custom fusion | bytes 12615680 | tf_op jit(solution)/shard_map/gather | solution.py:46
  428.5 0.0 copy-done.1
  428.5 0.0 slice-start
  428.5 0.1 compare_reduce_fusion
  428.6 0.0 slice-start.1
  428.6 7.1 fusion.12
  435.6 0.0 slice-done
  435.6 0.0 slice-done.1
  435.7 4.0 fusion.13
  439.7 26.9 %reduce-scatter.4.cloned.1.call-done = f32[4,768,768]{1,2,0:T(8,128)} async-done(((f32[4,768,3072]{1,2,0:T(8,128)}), f32[4,768,768]{1,2,0:T(8,128)}) %reduce-scatter.4.cloned.1.call-update) | async-done | bytes 9437200 | tf_op jit(solution)/shard_map/reduce_scatter | solution.py:48
  466.6 9.6 copy.34
  476.1 310.1 %reduce-scatter.6.cloned.1.call-done = f32[4,768,768]{1,2,0:T(8,128)} async-done(((f32[4,768,3072]{1,2,0:T(8,128)}), f32[4,768,768]{1,2,0:T(8,128)}) %reduce-scatter.6.cloned.1.call-update) | async-done | bytes 9437200 | tf_op jit(solution)/shard_map/reduce_scatter | solution.py:49
  786.2 9.6 copy.35
  795.8 310.7 %reduce-scatter.8.cloned.1.call-done = f32[4,768,768]{2,1,0:T(8,128)} async-done(((f32[4,3072,768]{2,1,0:T(8,128)}), f32[4,768,768]{2,1,0:T(8,128)}) %reduce-scatter.8.cloned.1.call-update) | async-done | bytes 9437200 | tf_op jit(solution)/shard_map/reduce_scatter | solution.py:50
  (2 shorter events, 0.0 us)
Async XLA Ops:
  7.2 459.4 %reduce-scatter.4.cloned.1.call-start = ((), (), s32[]{:S(2)}) async-start(), calls=%async_computation.5 | async-start | bytes 47185920 | tf_op jit(solution)/shard_map/reduce_scatter | solution.py:48
  147.3 638.9 %reduce-scatter.6.cloned.1.call-start = ((), (), s32[]{:S(2)}) async-start(), calls=%async_computation.6 | async-start | bytes 47185920 | tf_op jit(solution)/shard_map/reduce_scatter | solution.py:49
  182.7 923.9 %reduce-scatter.8.cloned.1.call-start = ((), (), s32[]{:S(2)}) async-start(), calls=%async_computation.7 | async-start | bytes 47185920 | tf_op jit(solution)/shard_map/reduce_scatter | solution.py:50
  293.2 13.7 %copy-start = (s32[4096,2]{0,1:T(2,128)S(1)}, s32[4096,2]{0,1:T(2,128)}, u32[]{:S(2)}) copy-start(s32[4096,2]{0,1:T(2,128)} %get-tuple-element.22) | copy-start | bytes 98308
  300.2 13.5 %all-to-all-start.1 = ((bf16[2,4,640,768]{3,2,1,0:T(8,128)(2,1)}), bf16[2,4,640,768]{3,2,1,0:T(8,128)(2,1)}, u32[]{:S(2)}, u32[]{:S(2)}) async-start(bf16[2,4,640,768]{3,2,1,0:T(8,128)(2,1)} %bitcast.38), calls=%async_computation.1 | async-start | bytes 15728640 | tf_op jit(solution)/shard_map/all_to_all | solution.py:45
  313.6 114.9 %copy-start.1 = (s32[4096,1]{0,1:T(1,128)S(1)}, s32[4096,1]{0,1:T(1,128)}, u32[]{:S(2)}) copy-start(s32[4096,1]{0,1:T(1,128)} %param.14) | copy-start | bytes 49156
  428.5 7.1 slice-start
  428.6 7.1 slice-start.1
Sparse Core Ops, SparseCore 0:
  147.4 319.0 reduce-scatter.3
  469.6 316.6 reduce-scatter.5
  789.9 316.6 reduce-scatter.7
where the time goes:
time: 1120 us; the launch traced here: 1110 us
  waiting for transfers between devices  654 us (58%)
  matrix products  243 us (22%)
  local copies, waits for them, and re-layouts  145 us (13%)
  other arithmetic  38.3 us (3%)
  between operations  14.3 us (1%)
  blocking collectives  12.4 us (1%)
    reduce_scatter x1, waiting for transfers between devices, body(): dw2 = lax.psum_scatter(dw2, 'data', scatter_dimension=1, tiled=True)  311 us
    reduce_scatter x1, waiting for transfers between devices, body(): dw3 = lax.psum_scatter(dw3, 'data', scatter_dimension=2, tiled=True)  310 us
    gather x1, local copies, waits for them, and re-layouts, body(): got = back[topk_idx, jnp.minimum(col, cap - 1)].astype(F32)  115 us
    dot_general x1, matrix products, _swiglu_bwd(): jnp.einsum('ecd,efd->ecf', dyd, w2, preferred_element_type=F32).astype(BF16)  61.6 us
    dot_general x1, matrix products, _swiglu_bwd(): dw2 = jnp.einsum('ecf,ecd->efd', a, dyd, preferred_element_type=F32)  45.8 us
    dot_general x1, matrix products, _swiglu_bwd(): dw1 = jnp.einsum('ecd,ecf->edf', xd, dh1, preferred_element_type=F32)  35.3 us
    dot_general x1, matrix products, _swiglu_bwd(): dw3 = jnp.einsum('ecd,ecf->edf', xd, dh3, preferred_element_type=F32)  35.3 us
    dot_general x1, matrix products, _swiglu_bwd(): jnp.einsum('ecf,edf->ecd', dh3, w3, preferred_element_type=F32)  32.9 us
  transfers between devices with their start and end apart: 4, of which 4 were waited for; matrix products, arithmetic and copies ran while one was open for 27% of the time, Pallas kernels for 0%

commit v1 on v0

v1 whole, which is shorter than its diff:
```python
import functools

import jax
import jax.numpy as jnp
from jax import lax
from jax.experimental import pallas as pl
from jax.experimental.pallas import tpu as pltpu
from jax.sharding import PartitionSpec as P

F32 = jnp.float32
BF16 = jnp.bfloat16
I32 = jnp.int32
RB = 256
AL = 32
VMEM_LIMIT = 62 * 1024 * 1024
ANY = pl.BlockSpec(memory_space=pl.ANY)


def _used(meta, ns, ne, el, g, j, r):
    e = meta[ns * ne]
    v = meta[(g * (ne // el) + jnp.bitwise_xor(e, r)) * ne + e * el + j]
    return jnp.bitwise_and(v + (AL - 1), -AL)


def _pack_kernel(dims, bounds, base_e, meta, src0, src1, *rest):
    ns, ne, el = dims
    nc = len(bounds) - 1
    outs, (lst, sem_in, sem_out) = rest[:nc], rest[nc:]
    total = bounds[-1]
    e = meta[ns * ne]
    d = meta[ns * ne + 1]

    def zero(i, c):
        lst[pl.ds(i * 64, 64), :] = jnp.zeros((64, lst.shape[1]), BF16)
        return c
    lax.fori_loop(0, total // 64, zero, 0)

    def walk(start):
        off = jnp.int32(0)
        for j in range(el):
            for r in range(2):
                src = (src0, src1)[r]
                n = _used(meta, ns, ne, el, d, j, r)
                cap = src0.shape[0] // el // (2 if base_e else 1)
                base = j * 2 * cap + jnp.bitwise_xor(e, r) * cap if base_e else jnp.int32(j * cap)
                nbig = n // 128
                for size, lo, cnt in ((128, 0, nbig), (AL, nbig * 128, (n - nbig * 128) // AL)):
                    def step(i, c, size=size, lo=lo, base=base, off=off, src=src):
                        p = lo + i * size
                        cp = pltpu.make_async_copy(src.at[pl.ds(pl.multiple_of(base + p, AL), size)],
                                                   lst.at[pl.ds(pl.multiple_of(off + p, AL), size)], sem_in)
                        if start:
                            cp.start()
                        else:
                            cp.wait()
                        return c
                    lax.fori_loop(0, cnt, step, 0)
                off = off + n
    walk(True)
    walk(False)
    cps = [pltpu.make_async_copy(lst.at[pl.ds(bounds[i], bounds[i + 1] - bounds[i])], outs[i], sem_out.at[i])
           for i in range(nc)]
    for cp in cps:
        cp.start()
    for cp in cps:
        cp.wait()


def _pack(meta, src0, src1, dims, bounds, base_e):
    w = src0.shape[1]
    nc = len(bounds) - 1
    return pl.pallas_call(
        functools.partial(_pack_kernel, dims, bounds, base_e),
        grid_spec=pltpu.PrefetchScalarGridSpec(
            num_scalar_prefetch=1, grid=(), in_specs=[ANY, ANY], out_specs=[ANY] * nc,
            scratch_shapes=[pltpu.VMEM((bounds[-1], w), BF16), pltpu.SemaphoreType.DMA, pltpu.SemaphoreType.DMA((nc,))]),
        out_shape=[jax.ShapeDtypeStruct((bounds[i + 1] - bounds[i], w), BF16) for i in range(nc)],
        compiler_params=pltpu.CompilerParams(vmem_limit_bytes=24 * 1024 * 1024),
        cost_estimate=pl.CostEstimate(flops=0, bytes_accessed=4 * bounds[-1] * w, transcendentals=0),
        name="pack",
    )(meta, src0, src1)


def _nt(a, b):
    return lax.dot_general(a, b, (((1,), (1,)), ((), ())), preferred_element_type=F32)


def _tn(a, b):
    return lax.dot_general(a, b, (((0,), (0,)), ((), ())), preferred_element_type=F32)


def _own_kernel(dims, cap, meta, g0, g1, h1, h3, w1, w3, w2, o0, o1, gb, h1b, h3b, acc, ob, items, sin, sout):
    ns, ne, el = dims
    j = pl.program_id(0)
    e = meta[ns * ne]
    d = meta[ns * ne + 1]
    ff = w1.shape[2]
    fc = w1.shape[1]

    cnt = jnp.int32(0)
    for r in range(2):
        n = _used(meta, ns, ne, el, d, j, r)
        nb = (n + RB - 1) // RB

        def put(b, c, r=r):
            items[c, 0] = r
            items[c, 1] = jnp.minimum(b * RB, cap - RB)
            return c + 1
        cnt = lax.fori_loop(0, nb, put, cnt)

    def copies(i, slot, op):
        r = items[i, 0]
        st = items[i, 1]
        row = pl.multiple_of(jnp.bitwise_xor(e, r) * cap + st, 128)
        for k, (src, dst) in enumerate(((h1, h1b), (h3, h3b))):
            op(pltpu.make_async_copy(src.at[j, pl.ds(row, RB)], dst.at[slot], sin.at[slot, k]))
        st = pl.multiple_of(st, 128)
        for q, g in enumerate((g0, g1)):
            @pl.when(r == q)
            def _():
                op(pltpu.make_async_copy(g.at[j, pl.ds(st, RB)], gb.at[slot], sin.at[slot, 2]))

    def out(i, slot, op):
        r = items[i, 0]
        st = pl.multiple_of(items[i, 1], 128)
        for q, o in enumerate((o0, o1)):
            @pl.when(r == q)
            def _():
                op(pltpu.make_async_copy(ob.at[slot], o.at[j, pl.ds(st, RB)], sout.at[slot]))

    start = lambda cp: cp.start()
    wait = lambda cp: cp.wait()

    @pl.when(cnt > 0)
    def _():
        copies(0, 0, start)

    def step(i, c):
        slot = lax.rem(i, 2)

        @pl.when(i + 1 < cnt)
        def _():
            copies(i + 1, 1 - slot, start)
        copies(i, slot, wait)
        @pl.when(i >= 1)
        def _():
            out(i - 1, 1 - slot, wait)
        g = gb[slot]

        def hid(k, c2):
            f = pl.multiple_of(k * fc, 128)
            da = _nt(g, w2[0, pl.ds(f, fc), :]).astype(BF16).astype(F32)
            h1f = h1b[slot, :, pl.ds(f, fc)].astype(F32)
            h3f = h3b[slot, :, pl.ds(f, fc)].astype(F32)
            s = jax.nn.sigmoid(h1f)
            dh1 = (da * h3f * s * (1.0 + h1f * (1.0 - s))).astype(BF16)
            dh3 = (da * (h1f * s)).astype(BF16)
            p = _nt(dh1, w1[0, :, pl.ds(f, fc)]) + _nt(dh3, w3[0, :, pl.ds(f, fc)])
            acc[...] = jnp.where(k == 0, p, acc[...] + p)
            return c2
        lax.fori_loop(0, ff // fc, hid, 0)
        ob[slot] = acc[...].astype(BF16)
        out(i, slot, start)
        return c
    lax.fori_loop(0, cnt, step, 0)

    @pl.when(cnt > 0)
    def _():
        out(cnt - 1, lax.rem(cnt - 1, 2), wait)


def _own(meta, g0, g1, h1, h3, w1, w3, w2, dims):
    el, cap, w = g0.shape
    ff = w1.shape[2]
    wspec = lambda a: pl.BlockSpec((1,) + a.shape[1:], lambda j, m: (j, 0, 0))
    return pl.pallas_call(
        functools.partial(_own_kernel, dims, cap),
        grid_spec=pltpu.PrefetchScalarGridSpec(
            num_scalar_prefetch=1, grid=(el,),
            in_specs=[ANY, ANY, ANY, ANY, wspec(w1), wspec(w3), wspec(w2)], out_specs=[ANY, ANY],
            scratch_shapes=[pltpu.VMEM((2, RB, w), BF16), pltpu.VMEM((2, RB, ff), BF16), pltpu.VMEM((2, RB, ff), BF16),
                            pltpu.VMEM((RB, w), F32), pltpu.VMEM((2, RB, w), BF16), pltpu.SMEM((16, 2), I32),
                            pltpu.SemaphoreType.DMA((2, 3)), pltpu.SemaphoreType.DMA((2,))]),
        out_shape=[jax.ShapeDtypeStruct(g0.shape, BF16)] * 2,
        compiler_params=pltpu.CompilerParams(vmem_limit_bytes=VMEM_LIMIT),
        cost_estimate=pl.CostEstimate(flops=4 * el * cap * w * ff * 3, bytes_accessed=el * (cap * ff * 4 + 3 * w * ff * 2), transcendentals=0),
        name="own",
    )(meta, g0, g1, h1, h3, w1, w3, w2)


def _share_kernel(dims, lo, first, meta, xs, gs, w1, w3, w2, *rest):
    ns, ne, el = dims
    if first:
        ins, rest = None, rest
    else:
        ins, rest = rest[:3], rest[3:]
    dw1, dw3, dw2, xb, gb, items, sin = rest
    j = pl.program_id(0)
    ng, c, w = xs.shape
    for k, o in enumerate((dw1, dw3, dw2)):
        o[...] = jnp.zeros_like(o) if first else ins[k][...]

    cnt = jnp.int32(0)
    for g in range(ng):
        pos = jnp.int32(0)
        for jj in range(el):
            n = _used(meta, ns, ne, el, g, jj, 0) + _used(meta, ns, ne, el, g, jj, 1)
            pos = pos + jnp.where(jj < j, n, 0)
        n = _used(meta, ns, ne, el, g, j, 0) + _used(meta, ns, ne, el, g, j, 1)
        a = jnp.clip(pos - lo, 0, c)
        z = jnp.clip(pos + n - lo, 0, c)

        def put(b, k, g=g, a=a, z=z):
            s = a + b * RB
            items[k, 0] = g
            items[k, 1] = jnp.minimum(s, c - RB)
            items[k, 2] = s
            items[k, 3] = jnp.minimum(s + RB, z)
            return k + 1
        cnt = lax.fori_loop(0, (z - a + RB - 1) // RB, put, cnt)

    def copies(i, slot, op):
        g = items[i, 0]
        st = pl.multiple_of(items[i, 1], AL)
        for k, (src, dst) in enumerate(((xs, xb), (gs, gb))):
            op(pltpu.make_async_copy(src.at[g, pl.ds(st, RB)], dst.at[slot], sin.at[slot, k]))

    start = lambda cp: cp.start()
    wait = lambda cp: cp.wait()

    @pl.when(cnt > 0)
    def _():
        copies(0, 0, start)

    def step(i, carry):
        slot = lax.rem(i, 2)

        @pl.when(i + 1 < cnt)
        def _():
            copies(i + 1, 1 - slot, start)
        copies(i, slot, wait)
        row = items[i, 1] + lax.broadcasted_iota(I32, (RB, w), 0)
        keep = (row >= items[i, 2]) & (row < items[i, 3])
        x = jnp.where(keep, xb[slot].astype(F32), 0.0).astype(BF16)
        g = jnp.where(keep, gb[slot].astype(F32), 0.0).astype(BF16)
        h1f = jnp.dot(x, w1[0], preferred_element_type=F32).astype(BF16).astype(F32)
        h3f = jnp.dot(x, w3[0], preferred_element_type=F32).astype(BF16).astype(F32)
        da = _nt(g, w2[0]).astype(BF16).astype(F32)
        s = jax.nn.sigmoid(h1f)
        silu = h1f * s
        a = (silu * h3f).astype(BF16)
        dh1 = (da * h3f * s * (1.0 + h1f * (1.0 - s))).astype(BF16)
        dh3 = (da * silu).astype(BF16)
        dw1[0] += _tn(x, dh1)
        dw3[0] += _tn(x, dh3)
        dw2[0] += _tn(a, g)
        return carry
    lax.fori_loop(0, cnt, step, 0)


def _share(meta, xs, gs, w1, w3, w2, prev, lo, dims):
    ns, ne, el = dims
    ng, c, w = xs.shape
    fs = w1.shape[2] // ng
    di = ns * ne + 1
    in_specs = [ANY, ANY,
                pl.BlockSpec((1, w, fs), lambda j, m: (j, 0, m[di])),
                pl.BlockSpec((1, w, fs), lambda j, m: (j, 0, m[di])),
                pl.BlockSpec((1, fs, w), lambda j, m: (j, m[di], 0))]
    acc = [pl.BlockSpec((1, w, fs), lambda j, m: (j, 0, 0)), pl.BlockSpec((1, w, fs), lambda j, m: (j, 0, 0)),
           pl.BlockSpec((1, fs, w), lambda j, m: (j, 0, 0))]
    first = prev is None
    args = (meta, xs, gs, w1, w3, w2) + (() if first else tuple(prev))
    return pl.pallas_call(
        functools.partial(_share_kernel, dims, lo, first),
        grid_spec=pltpu.PrefetchScalarGridSpec(
            num_scalar_prefetch=1, grid=(el,), in_specs=in_specs + ([] if first else acc), out_specs=acc,
            scratch_shapes=[pltpu.VMEM((2, RB, w), BF16), pltpu.VMEM((2, RB, w), BF16),
                            pltpu.SMEM((ng * (c // RB + 2), 4), I32), pltpu.SemaphoreType.DMA((2, 2))]),
        out_shape=[jax.ShapeDtypeStruct((el, w, fs), F32), jax.ShapeDtypeStruct((el, w, fs), F32),
                   jax.ShapeDtypeStruct((el, fs, w), F32)],
        input_output_aliases={} if first else {6: 0, 7: 1, 8: 2},
        compiler_params=pltpu.CompilerParams(vmem_limit_bytes=VMEM_LIMIT),
        cost_estimate=pl.CostEstimate(flops=8 * ng * c * w * fs, bytes_accessed=4 * ng * c * w, transcendentals=0),
        name="share",
    )(*args)


def _take_kernel(n0, tb, idx, d0, d1, o, buf, row):
    i = pl.program_id(0)
    n, w = d0.shape

    @pl.when(i == 0)
    def _():
        for k, s in enumerate((d0, d1)):
            def fill(b, c, k=k, s=s):
                buf[pl.ds(k * n + b * 64, 64), :] = s[pl.ds(b * 64, 64), :].astype(F32)
                return c
            lax.fori_loop(0, n // 64, fill, 0)
        buf[pl.ds(2 * n, 8), :] = jnp.zeros((8, w), F32)

    def step(t, c):
        for u in range(8):
            row[pl.ds(t * 8 + u, 1), :] = buf[pl.ds(idx[i * tb + t * 8 + u], 1), :]
        return c
    lax.fori_loop(0, tb // 8, step, 0)
    o[...] = row[...].astype(BF16)


def _take(idx, d0, d1, tb=512):
    n, w = d0.shape
    t = idx.shape[0]
    whole = pl.BlockSpec((n, w), lambda i, m: (0, 0), pipeline_mode=pl.Buffered(1))
    return pl.pallas_call(
        functools.partial(_take_kernel, n, tb),
        grid_spec=pltpu.PrefetchScalarGridSpec(
            num_scalar_prefetch=1, grid=(t // tb,), in_specs=[whole, whole],
            out_specs=pl.BlockSpec((tb, w), lambda i, m: (i, 0)),
            scratch_shapes=[pltpu.VMEM((2 * n + 8, w), F32), pltpu.VMEM((tb, w), F32)]),
        out_shape=jax.ShapeDtypeStruct((t, w), BF16),
        compiler_params=pltpu.CompilerParams(vmem_limit_bytes=48 * 1024 * 1024),
        cost_estimate=pl.CostEstimate(flops=20 * t * w, bytes_accessed=8 * n * w, transcendentals=0),
        name="take",
    )(idx, d0, d1)


def solution(mesh):
    np_ = mesh.shape['expert']
    nd = mesh.shape['data']
    tok = P(('data', 'expert'), None)
    buf = P(('data', 'expert'), None, None)
    wsp = P('expert', None, None)

    def body(dy, gates, topk_idx, slot, yd, xd, h1, h3, w1, w3, w2):
        t, d = dy.shape
        el = w1.shape[0]
        ne = np_ * el
        ns = nd * np_
        cap = xd.shape[1] // np_
        dims = (ns, ne, el)
        e = lax.axis_index('expert')
        dd = lax.axis_index('data')
        ex = topk_idx[:, 0]
        sl = slot[:, 0]
        hit = (ex[None, :] == jnp.arange(ne, dtype=I32)[:, None]) & (sl >= 0)[None, :]
        used = jnp.max(jnp.where(hit, sl[None, :] + 1, 0), axis=1).astype(I32)
        alld = lax.all_gather(used, ('data', 'expert'), axis=0, tiled=True)
        meta = jnp.concatenate([alld, e[None].astype(I32), dd[None].astype(I32)])
        rows = jnp.bitwise_and(alld + (AL - 1), -AL).reshape(nd, np_, np_, el).sum(axis=(1, 3))
        most = jnp.max(rows)
        rel = jnp.bitwise_xor(ex, e.astype(I32) * el)
        flat = jnp.where(sl >= 0, rel * cap + sl, ne * cap)

        def path(bounds, dy, gates, flat, yd, xd, h1, h3, w1, w3, w2, meta):
            x2 = xd.reshape(el * np_ * cap, d)
            xl = _pack(meta, x2, x2, dims, bounds, True)
            v = (gates * dy.astype(F32)).astype(BF16)
            send = jnp.zeros((ne * cap, d), BF16).at[flat].set(v, mode='drop').reshape(2, el, cap, d)
            g0 = send[0]
            g1 = lax.ppermute(send[1], 'expert', [(0, 1), (1, 0)])
            gl = _pack(meta, g0.reshape(el * cap, d), g1.reshape(el * cap, d), dims, bounds, False)
            xa, ga = [], []
            dep = None
            for k in range(len(bounds) - 1):
                xk = xl[k]
                if k > 0:
                    xk, _ = lax.optimization_barrier((xk, gl[k - 1]))
                xa.append(lax.all_gather(xk, 'data'))
                ga.append(lax.all_gather(gl[k], 'data'))
            o0, o1 = _own(meta, g0, g1, h1, h3, w1, w3, w2, dims)
            b1 = lax.ppermute(o1, 'expert', [(0, 1), (1, 0)])
            dx = _take(flat, o0.reshape(el * cap, d), b1.reshape(el * cap, d))
            dg = jnp.einsum('tkd,td->tk', yd, dy, preferred_element_type=F32)
            acc = None
            for k in range(len(bounds) - 1):
                acc = _share(meta, xa[k], ga[k], w1, w3, w2, acc, bounds[k], dims)
            return dx, dg, acc[0], acc[1], acc[2]

        small = (0, 1280, 2304, 3328)
        large = (0, 2560, 5120)
        ops = (dy, gates, flat, yd, xd, h1, h3, w1, w3, w2, meta)
        return lax.cond(most <= small[-1], functools.partial(path, small), functools.partial(path, large), *ops)

    return jax.shard_map(body, mesh=mesh,
                         in_specs=(tok, tok, tok, tok, buf, buf, buf, buf, wsp, wsp, wsp),
                         out_specs=(tok, tok, P('expert', None, 'data'), P('expert', None, 'data'), P('expert', 'data', None)),
                         check_vma=False)
```

time: 1120 us -> 692 us (0.62)
  waiting for transfers between devices: 654 us -> 269 us
  Pallas kernels: 0 us -> 312 us
  matrix products: 243 us -> 0 us
  local copies, waits for them, and re-layouts: 145 us -> 16 us
  blocking collectives: 12.4 us -> 25 us
    reduce_scatter x3 -> x0, waiting for transfers between devices: 648 us -> none  [the longest x1 311 us: body(): dw2 = lax.psum_scatter(dw2, 'data', scatter_dimension=1, tiled=True)]
    pallas_call x0 -> x6, Pallas kernels: none -> 312 us  [the longest x2 155 us: _share(): pl.pallas_call(functools.partial(_share_kernel, dims, lo, first), grid_sp...]
    all_gather x0 -> x4, waiting for transfers between devices: none -> 261 us  [the longest x2 230 us: path(): ga.append(lax.all_gather(gl[k], 'data'))]
    dot_general x6 -> x0, matrix products: 243 us -> none  [the longest x1 61.6 us: _swiglu_bwd(): jnp.einsum('ecd,efd->ecf', dyd, w2, preferred_element_type=F32).astype(BF16)]
    gather x1 -> x0, local copies, waits for them, and re-layouts: 115 us -> none  [body(): got = back[topk_idx, jnp.minimum(col, cap - 1)].astype(F32)]
    unnamed x0 -> x1, blocking collectives: none -> 25 us
    scatter x0 -> x1, other arithmetic: none -> 25 us  [path(): jnp.zeros((ne * cap, d), BF16).at[flat].set(v, mode='drop')]
    unnamed x4 -> x0, other arithmetic: 25 us -> none
  transfers between devices with their start and end apart: 4 -> 6, of which waited for: 4 -> 5; matrix products, arithmetic and copies ran while one was open for 27% -> 5% of each run, Pallas kernels for 0% -> 39%
where the time goes in v1:
time: 692 us; the launch traced here: 680 us
  Pallas kernels  312 us (45%)
  waiting for transfers between devices  269 us (39%)
  other arithmetic  34.7 us (5%)
  blocking collectives  25 us (4%)
  local copies, waits for them, and re-layouts  16 us (2%)
  between operations  14.9 us (2%)
  loops' own time  8.25 us (1%)
    all_gather x2, waiting for transfers between devices, path(): ga.append(lax.all_gather(gl[k], 'data'))  230 us
    pallas_call x2, Pallas kernels, _share(): pl.pallas_call(functools.partial(_share_kernel, dims, lo, first), grid_sp...  155 us
    pallas_call x1, Pallas kernels, _own(): pl.pallas_call(functools.partial(_own_kernel, dims, cap), grid_spec=pltpu...  120 us
    all_gather x2, waiting for transfers between devices, path(): xa.append(lax.all_gather(xk, 'data'))  30.6 us
    pallas_call x1, Pallas kernels, _take(): pl.pallas_call(functools.partial(_take_kernel, n, tb), grid_spec=pltpu.Pr...  25.5 us
    unnamed x1, blocking collectives  25 us
    scatter x1, other arithmetic, path(): jnp.zeros((ne * cap, d), BF16).at[flat].set(v, mode='drop')  25 us
  transfers between devices with their start and end apart: 6, of which 5 were waited for; matrix products, arithmetic and copies ran while one was open for 5% of the time, Pallas kernels for 39%

profile of v1, /device:TPU:0, one launch (start us, length us, event | category | flops | bytes accessed | tf_op | source)
XLA Modules:
  0.0 680.1 jit_solution(3659887271518689988)
XLA Ops:
  7.2 0.7 broadcast_compare_fusion
  7.9 0.7 broadcast_add_fusion
  8.6 0.9 select_reduce_fusion
  9.5 0.2 dynamic-update-slice
  9.7 25.0 %all-reduce = s32[64]{0:T(128)S(1)} all-reduce(s32[64]{0:T(128)S(1)} %dynamic-update-slice), channel_id=1, replica_groups=mesh['data'=4,'expert'=2] {'data','expert'}, use_global_device_ids=true, to_apply=%add | all-reduce | flops 64 | bytes 512
  34.8 0.1 pad_add_fusion
  34.9 0.1 reshape.70
  35.0 0.2 reduce_sum.9
  35.1 0.6 reduce_max.19
  36.4 636.0 %conditional.1 = (f32[4,768,768]{2,1,0:T(8,128)}, f32[4,768,768]{2,1,0:T(8,128)}, f32[4,768,768]{2,1,0:T(8,128)}, bf16[4096,768]{1,0:T(8,128)(2,1)}, f32[4096,1]{0,1:T(1,128)S(1)}) conditional(s32[]{:T(128)} %convert_element_type.15, (pred[4096]{0:T(1024)(128)(4,1)S(1)}, f32[4096,1]{0,1:T(1,128)}, bf16[4096,768]{1,0:T(8,128)(2,1)}, s32[66]{0:T(128)S(1)}, ...), branch_computations={%region_3.5_spmd, %region_5.7_spmd} | conditional | flops 169199304704 | bytes 634163776 | solution.py:382
  36.4 0.0 all-gather.25.cloned.1.call-start
  36.5 0.0 copy-start.12
  36.5 0.0 copy-start.14
  36.5 0.0 copy-start.16
  36.5 4.0 pack.4
  40.5 0.0 copy-start.2
  40.5 1.9 copy-done.2
  42.4 0.0 copy-start.3
  42.4 1.9 copy-done.3
  44.3 0.0 all-gather.25.cloned.1.call-update
  44.4 0.0 all-gather.27.cloned.1.call-start
  44.4 0.0 copy-done.12
  44.4 0.0 copy-done.14
  44.5 0.0 copy-done.16
  44.5 25.0 %scatter_custom_fusion = bf16[5120,768]{1,0:T(8,128)(2,1)} fusion(s32[4096]{0:T(1024)S(1)} %get-tuple-element.208, bf16[4096,768]{1,0:T(8,128)(2,1)} %get-tuple-element.137, f32[4096]{0:T(1024)S(1)} %bitcast.59, bf16[]{:T(256)} %constant.14.clone), kind=kCustom, calls=%fused_computation.6 | custom fusion | flops 9437184 | bytes 14172162 | tf_op jit(solution)/shard_map/cond/branch_0_fun/scatter | solution.py:358
  69.5 3.6 fusion.19
  73.1 0.0 collective-permute-start
  73.1 6.8 collective-permute-done.g1
  79.9 0.0 copy-start.7
  79.9 7.3 %pack.5 = (bf16[2560,768]{1,0:T(8,128)(2,1)S(1)}, bf16[2560,768]{1,0:T(8,128)(2,1)S(1)}) custom-call(s32[66]{0:T(128)S(1)} %get-tuple-element.45.meta, bf16[2560,768]{1,0:T(8,128)(2,1)S(1)} %get-tuple-element.213.src0, bf16[2560,768]{1,0:T(8,128)(2,1)S(1)} %bitcast.37), custom_call_target="tpu_custom_call" | custom-call | bytes 15728640 | tf_op jit(solution)/shard_map/cond/branch_0_fun/pack/pallas_call | solution.py:72
  87.2 0.0 copy-done.7
  87.2 0.0 copy-start.1
  87.2 1.9 copy-done.1
  89.1 0.0 copy-start.4
  89.1 1.9 copy-done.4
  91.0 0.0 copy-start.6
  91.0 1.9 copy-done.6
  93.0 0.0 all-gather.27.cloned.1.call-update
  93.0 0.0 all-gather.21.cloned.1.call-start
  93.0 0.7 all-gather.21.cloned.1.call-update
  93.7 0.2 all-gather.23.cloned.1.call-start
  93.9 0.3 all-gather.23.cloned.1.call-update
  94.3 120.5 %own.2 = (bf16[4,640,768]{2,1,0:T(8,128)(2,1)}, bf16[4,640,768]{2,1,0:T(8,128)(2,1)}) custom-call(s32[66]{0:T(128)S(1)} %get-tuple-element.45.meta, bf16[4,640,768]{2,1,0:T(8,128)(2,1)} %bitcast.35, bf16[4,640,768]{2,1,0:T(8,128)(2,1)} %copy-done.7, bf16[4,1280,3072]{2,1,0:T(8,128)(2,1)} %get-tuple-element.139.h1, ...), custom_call_target="tpu_custom_call" | custom-call | flops 72477573120 | bytes 88080384 | tf_op jit(solution)/shard_map/cond/branch_0_fun/own/pallas_call | solution.py:176
  214.8 0.0 copy-start.8
  214.8 0.0 collective-permute-start.1
  214.8 6.5 fusion.1
  221.3 0.3 collective-permute-done.1
  221.6 0.0 copy-start.10
  221.6 1.9 copy-done.10
  223.5 0.0 copy-done.8
  223.5 25.5 %take.2 = bf16[4096,768]{1,0:T(8,128)(2,1)} custom-call(s32[4096]{0:T(1024)S(1)} %get-tuple-element.209.idx, bf16[2560,768]{1,0:T(8,128)(2,1)S(1)} %bitcast.38, bf16[2560,768]{1,0:T(8,128)(2,1)} %bitcast.48), custom_call_target="tpu_custom_call" | custom-call | flops 62914560 | bytes 15728640 | tf_op jit(solution)/shard_map/cond/branch_0_fun/take/pallas_call | solution.py:314
  249.0 0.0 all-gather.25.cloned.1.call-done
  249.0 85.5 %all-gather.27.cloned.1.call-done = bf16[10240,768]{1,0:T(8,128)(2,1)} async-done(((bf16[2560,768]{1,0:T(8,128)(2,1)}), bf16[10240,768]{1,0:T(8,128)(2,1)}) %all-gather.27.cloned.1.call-update) | async-done | bytes 15728656 | tf_op jit(solution)/shard_map/cond/branch_0_fun/all_gather | solution.py:369
  334.5 114.3 %share.5 = (f32[4,768,768]{2,1,0:T(8,128)}, f32[4,768,768]{2,1,0:T(8,128)}, f32[4,768,768]{2,1,0:T(8,128)}) custom-call(s32[66]{0:T(128)S(1)} %get-tuple-element.45.meta, bf16[4,2560,768]{2,1,0:T(8,128)(2,1)} %bitcast.63, bf16[4,2560,768]{2,1,0:T(8,128)(2,1)} %bitcast.65, bf16[4,768,3072]{2,1,0:T(8,128)(2,1)} %get-tuple-element.143.w1, ...), custom_call_target="tpu_custom_call" | custom-call | flops 48318382080 | bytes 31457280 | tf_op jit(solution)/shard_map/cond/branch_0_fun/share/pallas_call | solution.py:274
  448.8 30.6 %all-gather.21.cloned.1.call-done = bf16[10240,768]{1,0:T(8,128)(2,1)} async-done(((bf16[2560,768]{1,0:T(8,128)(2,1)}), bf16[10240,768]{1,0:T(8,128)(2,1)}) %all-gather.21.cloned.1.call-update) | async-done | bytes 15728656 | tf_op jit(solution)/shard_map/cond/branch_0_fun/all_gather | solution.py:368
  479.4 144.7 %all-gather.23.cloned.1.call-done = bf16[10240,768]{1,0:T(8,128)(2,1)} async-done(((bf16[2560,768]{1,0:T(8,128)(2,1)}), bf16[10240,768]{1,0:T(8,128)(2,1)}) %all-gather.23.cloned.1.call-update) | async-done | bytes 15728656 | tf_op jit(solution)/shard_map/cond/branch_0_fun/all_gather | solution.py:369
  624.1 40.3 %share.6 = (f32[4,768,768]{2,1,0:T(8,128)}, f32[4,768,768]{2,1,0:T(8,128)}, f32[4,768,768]{2,1,0:T(8,128)}) custom-call(s32[66]{0:T(128)S(1)} %get-tuple-element.45.meta, bf16[4,2560,768]{2,1,0:T(8,128)(2,1)} %bitcast.64, bf16[4,2560,768]{2,1,0:T(8,128)(2,1)} %bitcast.66, ...), custom_call_target="tpu_custom_call", output_to_operand_aliasing={{0}: (6, {}), {1}: (7, {}), {2}: (8, {})} | custom-call | flops 48318382080 | bytes 31457280 | tf_op jit(solution)/shard_map/cond/branch_0_fun/share/pallas_call | solution.py:274
  672.4 0.0 copy-start.18
  672.5 0.6 copy-done.18
  (3 shorter events, 0.0 us)
Async XLA Ops:
  36.4 212.6 %all-gather.25.cloned.1.call-start = ((), (), s32[]{:S(2)}) async-start(), calls=%async_computation.2 | async-start | bytes 19660800 | tf_op jit(solution)/shard_map/cond/branch_0_fun/all_gather | solution.py:368
  36.5 8.0 %copy-start.12 = (s32[4096]{0:T(1024)S(1)}, s32[4096]{0:T(1024)}, u32[]{:S(2)}) copy-start(s32[4096]{0:T(1024)} %get-tuple-element.130) | copy-start | bytes 49156 | tf_op jit(solution)/shard_map/cond
  36.5 8.0 %copy-start.14 = (s32[4096]{0:T(1024)S(1)}, s32[4096]{0:T(1024)}, u32[]{:S(2)}) copy-start(s32[4096]{0:T(1024)} %get-tuple-element.157) | copy-start | bytes 49156 | tf_op jit(solution)/shard_map/cond
  36.5 8.0 %copy-start.16 = (f32[4096,1]{0,1:T(1,128)S(1)}, f32[4096,1]{0,1:T(1,128)}, u32[]{:S(2)}) copy-start(f32[4096,1]{0,1:T(1,128)} %get-tuple-element.135) | copy-start | bytes 49156 | tf_op jit(solution)/shard_map/cond
  40.5 1.9 copy-start.2
  42.4 1.9 copy-start.3
  44.4 290.1 %all-gather.27.cloned.1.call-start = ((), (), s32[]{:S(2)}) async-start(), calls=%async_computation.3 | async-start | bytes 19660800 | tf_op jit(solution)/shard_map/cond/branch_0_fun/all_gather | solution.py:369
  73.1 6.8 %collective-permute-start = (bf16[4,640,768]{2,1,0:T(8,128)(2,1)S(1)}, bf16[4,640,768]{2,1,0:T(8,128)(2,1)S(1)}, u32[]{:S(2)}, u32[]{:S(2)}) collective-permute-start(bf16[4,640,768]{2,1,0:T(8,128)(2,1)S(1)} %bitcast.50), channel_id=1, source_target_pairs={{0,1},{1,0},{2,3},{3,2},{4,5},{5,4},{6,7},{7,6}} | collective-permute-start | bytes 11796488 | tf_op jit(solution)/shard_map/cond/branch_0_fun/ppermute | solution.py:360
  79.9 7.3 %copy-start.7 = (bf16[4,640,768]{2,1,0:T(8,128)(2,1)}, bf16[4,640,768]{2,1,0:T(8,128)(2,1)S(1)}, u32[]{:S(2)}) copy-start(bf16[4,640,768]{2,1,0:T(8,128)(2,1)S(1)} %collective-permute-done.g1) | copy-start | bytes 11796484 | tf_op jit(solution)/shard_map/cond
  87.2 1.9 copy-start.1
  89.1 1.9 copy-start.4
  91.0 1.9 copy-start.6
  93.0 386.4 %all-gather.21.cloned.1.call-start = ((), (), s32[]{:S(2)}) async-start(), calls=%async_computation | async-start | bytes 19660800 | tf_op jit(solution)/shard_map/cond/branch_0_fun/all_gather | solution.py:368
  93.7 530.4 %all-gather.23.cloned.1.call-start = ((), (), s32[]{:S(2)}) async-start(), calls=%async_computation.1 | async-start | bytes 19660800 | tf_op jit(solution)/shard_map/cond/branch_0_fun/all_gather | solution.py:369
  214.8 8.7 %copy-start.8 = (bf16[4,640,768]{2,1,0:T(8,128)(2,1)S(1)}, bf16[4,640,768]{2,1,0:T(8,128)(2,1)}, u32[]{:S(2)}) copy-start(bf16[4,640,768]{2,1,0:T(8,128)(2,1)} %get-tuple-element.53) | copy-start | bytes 11796484 | tf_op jit(solution)/shard_map/cond
  214.8 6.8 %collective-permute-start.1 = (bf16[4,640,768]{2,1,0:T(8,128)(2,1)}, bf16[4,640,768]{2,1,0:T(8,128)(2,1)S(1)}, u32[]{:S(2)}, u32[]{:S(2)}) collective-permute-start(bf16[4,640,768]{2,1,0:T(8,128)(2,1)} %get-tuple-element.54), channel_id=1, source_target_pairs={{0,1},{1,0},{2,3},{3,2},{4,5},{5,4},{6,7},{7,6}} | collective-permute-start | bytes 11796488 | tf_op jit(solution)/shard_map/cond/branch_0_fun/ppermute | solution.py:371
  221.6 1.9 copy-start.10
  672.4 0.6 copy-start.18
Sparse Core Ops, SparseCore 0:
  44.5 144.4 all-gather.24
  191.4 143.0 all-gather.26
  336.2 143.0 all-gather.20
  481.0 143.0 all-gather.22

commit v2 on v1

v2 whole, which is shorter than its diff:
```python
import functools

import jax
import jax.numpy as jnp
from jax import lax
from jax.experimental import pallas as pl
from jax.experimental.pallas import tpu as pltpu
from jax.sharding import PartitionSpec as P


F32 = jnp.float32
BF16 = jnp.bfloat16
I32 = jnp.int32
RB = 256
AL = 16
VMEM_LIMIT = 62 * 1024 * 1024
ANY = pl.BlockSpec(memory_space=pl.ANY)


def _used(meta, dims, g, j, r, other=0):
    ns, ne, el = dims
    e = jnp.bitwise_xor(meta[ns * ne], other)
    v = meta[(g * (ne // el) + jnp.bitwise_xor(e, r)) * ne + e * el + j]
    return jnp.bitwise_and(v + (AL - 1), -AL)


def _total(meta, dims, g):
    n = jnp.int32(0)
    for j in range(dims[2]):
        n = n + _used(meta, dims, g, j, 0) + _used(meta, dims, g, j, 1)
    return n


def _pack_kernel(dims, bounds, win, base_e, meta, src0, src1, *rest):
    ns, ne, el = dims
    nc = len(bounds) - 1 + (1 if win else 0)
    outs, (lst, sem_in, sem_out) = rest[:nc], rest[nc:]
    e = meta[ns * ne]
    d = meta[ns * ne + 1]

    def zero(i, c):
        lst[pl.ds(i * 64, 64), :] = jnp.zeros((64, lst.shape[1]), BF16)
        return c

    lax.fori_loop(0, lst.shape[0] // 64, zero, 0)

    def walk(start):
        off = jnp.int32(0)
        for j in range(el):
            for r in range(2):
                src = (src0, src1)[r]
                n = _used(meta, dims, d, j, r)
                cap = src0.shape[0] // el // (2 if base_e else 1)
                base = j * 2 * cap + jnp.bitwise_xor(e, r) * cap if base_e else jnp.int32(j * cap)
                nbig = n // 128
                for size, lo, cnt in ((128, 0, nbig), (AL, nbig * 128, (n - nbig * 128) // AL)):
                    def step(i, c, size=size, lo=lo, base=base, off=off, src=src):
                        p = lo + i * size
                        cp = pltpu.make_async_copy(src.at[pl.ds(pl.multiple_of(base + p, AL), size)],
                                                   lst.at[pl.ds(pl.multiple_of(off + p, AL), size)], sem_in)
                        if start:
                            cp.start()
                        else:
                            cp.wait()
                        return c

                    lax.fori_loop(0, cnt, step, 0)
                off = off + n
        return off

    walk(True)
    total = walk(False)
    cps = [pltpu.make_async_copy(lst.at[pl.ds(bounds[i], bounds[i + 1] - bounds[i])], outs[i], sem_out.at[i])
           for i in range(len(bounds) - 1)]
    if win:
        st = pl.multiple_of(jnp.clip(total - win, 0, lst.shape[0] - win), AL)
        cps.append(pltpu.make_async_copy(lst.at[pl.ds(st, win)], outs[nc - 1], sem_out.at[nc - 1]))
    for cp in cps:
        cp.start()
    for cp in cps:
        cp.wait()


def _pack(meta, src0, src1, dims, bounds, win, base_e):
    w = src0.shape[1]
    sizes = [b - a for a, b in zip(bounds, bounds[1:])] + ([win] if win else [])
    nc = len(sizes)
    rows = bounds[-1] + win
    return pl.pallas_call(
        functools.partial(_pack_kernel, dims, bounds, win, base_e),
        grid_spec=pltpu.PrefetchScalarGridSpec(
            num_scalar_prefetch=1, grid=(), in_specs=[ANY, ANY], out_specs=[ANY] * nc,
            scratch_shapes=[pltpu.VMEM((rows, w), BF16), pltpu.SemaphoreType.DMA, pltpu.SemaphoreType.DMA((nc,))]),
        out_shape=[jax.ShapeDtypeStruct((n, w), BF16) for n in sizes],
        compiler_params=pltpu.CompilerParams(vmem_limit_bytes=24 * 1024 * 1024),
        cost_estimate=pl.CostEstimate(flops=0, bytes_accessed=4 * rows * w, transcendentals=0),
        name="pack",
    )(meta, src0, src1)


def _extent_kernel(mesh_shape, ne, ex, sl, o, mine, sem_local, ssem, rsem):
    nd, npar = mesh_shape
    d = lax.axis_index('data')
    e = lax.axis_index('expert')
    lane = lax.broadcasted_iota(I32, (8, 128), 1)
    vec = jnp.zeros((8, 128), I32)
    idx = ex[...]
    pos = sl[...]
    for k in range(ne):
        top = jnp.max(jnp.where((idx == k) & (pos >= 0), pos + 1, 0))
        vec = jnp.where(lane == k, top, vec)
    mine[...] = vec
    bar = pltpu.get_barrier_semaphore()
    peers = [(a, b) for a in range(nd) for b in range(npar) if a or b]
    dev = lambda a, b: (jnp.bitwise_xor(d, a), jnp.bitwise_xor(e, b))
    for a, b in peers:
        pl.semaphore_signal(bar, inc=1, device_id=dev(a, b), device_id_type=pl.DeviceIdType.MESH)
    pl.semaphore_wait(bar, len(peers))
    me = d * npar + e
    cps = []
    for k, (a, b) in enumerate(peers):
        cp = pltpu.make_async_remote_copy(mine, o.at[me], ssem.at[k], rsem.at[k], device_id=dev(a, b),
                                          device_id_type=pl.DeviceIdType.MESH)
        cp.start()
        cps.append(cp)
    own = pltpu.make_async_copy(mine, o.at[me], sem_local)
    own.start()
    own.wait()
    for cp in cps:
        cp.wait()


def _extents(ex, sl, ne, mesh_shape):
    nd, npar = mesh_shape
    n = nd * npar
    rows = ex.shape[0] // 128
    vm = pl.BlockSpec(memory_space=pltpu.VMEM)
    out = pl.pallas_call(
        functools.partial(_extent_kernel, mesh_shape, ne),
        in_specs=[vm, vm], out_specs=vm,
        scratch_shapes=[pltpu.VMEM((8, 128), I32), pltpu.SemaphoreType.DMA, pltpu.SemaphoreType.DMA((n - 1,)),
                        pltpu.SemaphoreType.DMA((n - 1,))],
        out_shape=jax.ShapeDtypeStruct((n, 8, 128), I32),
        compiler_params=pltpu.CompilerParams(collective_id=0, has_side_effects=True),
        cost_estimate=pl.CostEstimate(flops=0, bytes_accessed=65536, transcendentals=0),
        name="extents",
    )(ex.reshape(rows, 128), sl.reshape(rows, 128))
    return out[:, 0, :ne].reshape(n * ne)


def _nt(a, b):
    return lax.dot_general(a, b, (((1,), (1,)), ((), ())), preferred_element_type=F32)


def _tn(a, b):
    return lax.dot_general(a, b, (((0,), (0,)), ((), ())), preferred_element_type=F32)


def _own_kernel(dims, cap, meta, g0, g1, h1, h3, w1, w3, w2, o0, o1, gb, h1b, h3b, ob, items, sin, sout):
    ns, ne, _ = dims
    j = pl.program_id(0)
    e = meta[ns * ne]
    d = meta[ns * ne + 1]
    ff = w1.shape[2]
    fc = w1.shape[1]

    cnt = jnp.int32(0)
    for r in range(2):
        n = _used(meta, dims, d, j, r)
        nb = (n + RB - 1) // RB

        def put(b, c, r=r):
            items[c, 0] = r
            items[c, 1] = jnp.minimum(b * RB, cap - RB)
            return c + 1

        cnt = lax.fori_loop(0, nb, put, cnt)

    def copies(i, slot, op):
        r = items[i, 0]
        st = items[i, 1]
        row = pl.multiple_of(jnp.bitwise_xor(e, r) * cap + st, 128)
        for k, (src, dst) in enumerate(((h1, h1b), (h3, h3b))):
            op(pltpu.make_async_copy(src.at[j, pl.ds(row, RB)], dst.at[slot], sin.at[slot, k]))
        st = pl.multiple_of(st, 128)
        for q, g in enumerate((g0, g1)):
            @pl.when(r == q)
            def _():
                op(pltpu.make_async_copy(g.at[j, pl.ds(st, RB)], gb.at[slot], sin.at[slot, 2]))

    def out(i, slot, op):
        r = items[i, 0]
        st = pl.multiple_of(items[i, 1], 128)
        for q, o in enumerate((o0, o1)):
            @pl.when(r == q)
            def _():
                op(pltpu.make_async_copy(ob.at[slot], o.at[j, pl.ds(st, RB)], sout.at[slot]))

    start = lambda cp: cp.start()
    wait = lambda cp: cp.wait()

    @pl.when(cnt > 0)
    def _():
        copies(0, 0, start)

    def step(i, c):
        slot = lax.rem(i, 2)

        @pl.when(i + 1 < cnt)
        def _():
            copies(i + 1, 1 - slot, start)

        copies(i, slot, wait)

        @pl.when(i >= 1)
        def _():
            out(i - 1, 1 - slot, wait)

        g = gb[slot]

        p = None
        for k in range(ff // fc):
            f = k * fc
            da = _nt(g, w2[0, f:f + fc, :]).astype(BF16).astype(F32)
            h1f = h1b[slot, :, f:f + fc].astype(F32)
            h3f = h3b[slot, :, f:f + fc].astype(F32)
            s = 0.5 * jnp.tanh(0.5 * h1f) + 0.5
            silu = h1f * s
            dh1 = (da * h3f * (s + silu * (1.0 - s))).astype(BF16)
            dh3 = (da * silu).astype(BF16)
            q = _nt(dh1, w1[0, :, f:f + fc]) + _nt(dh3, w3[0, :, f:f + fc])
            p = q if p is None else p + q
        ob[slot] = p.astype(BF16)
        out(i, slot, start)
        return c

    lax.fori_loop(0, cnt, step, 0)

    @pl.when(cnt > 0)
    def _():
        out(cnt - 1, lax.rem(cnt - 1, 2), wait)


def _own(meta, g0, g1, h1, h3, w1, w3, w2, dims):
    el, cap, w = g0.shape
    ff = w1.shape[2]
    wspec = lambda a: pl.BlockSpec((1,) + a.shape[1:], lambda j, m: (j, 0, 0))
    return pl.pallas_call(
        functools.partial(_own_kernel, dims, cap),
        grid_spec=pltpu.PrefetchScalarGridSpec(
            num_scalar_prefetch=1, grid=(el,),
            in_specs=[ANY, ANY, ANY, ANY, wspec(w1), wspec(w3), wspec(w2)], out_specs=[ANY, ANY],
            scratch_shapes=[pltpu.VMEM((2, RB, w), BF16), pltpu.VMEM((2, RB, ff), BF16), pltpu.VMEM((2, RB, ff), BF16),
                            pltpu.VMEM((2, RB, w), BF16), pltpu.SMEM((16, 2), I32),
                            pltpu.SemaphoreType.DMA((2, 3)), pltpu.SemaphoreType.DMA((2,))]),
        out_shape=[jax.ShapeDtypeStruct(g0.shape, BF16)] * 2,
        compiler_params=pltpu.CompilerParams(vmem_limit_bytes=VMEM_LIMIT),
        cost_estimate=pl.CostEstimate(flops=4 * el * cap * w * ff * 3, bytes_accessed=el * (cap * ff * 4 + 3 * w * ff * 2), transcendentals=0),
        name="own",
    )(meta, g0, g1, h1, h3, w1, w3, w2)


def _share_kernel(dims, parts, first, meta, *rest):
    ns, ne, el = dims
    na = len(parts)
    arrs, rest = rest[:2 * na], rest[2 * na:]
    (w1, w3, w2), rest = rest[:3], rest[3:]
    if first:
        ins = None
    else:
        ins, rest = rest[:3], rest[3:]
    dw1, dw3, dw2, xb, gb, items, sin = rest
    j = pl.program_id(0)
    w = w1.shape[1]
    ng = ns * el // ne
    for k, o in enumerate((dw1, dw3, dw2)):
        o[...] = jnp.zeros_like(o) if first else ins[k][...]

    cnt = jnp.int32(0)
    for g in range(ng):
        pos = jnp.int32(0)
        for jj in range(el):
            n = _used(meta, dims, g, jj, 0) + _used(meta, dims, g, jj, 1)
            pos = pos + jnp.where(jj < j, n, 0)
        n = _used(meta, dims, g, j, 0) + _used(meta, dims, g, j, 1)
        for q, (pre, lo, hi, c) in enumerate(parts):
            if hi is None:
                base = _total(meta, dims, g) - c
                a = jnp.maximum(pos, lo) - base
                z = pos + n - base
            else:
                a = jnp.clip(pos - lo, 0, c)
                z = jnp.clip(pos + n - lo, 0, c)

            def put(b, k, q=q, g=g, a=a, z=z, c=c):
                s = a + b * RB
                items[k, 0] = q
                items[k, 1] = g
                items[k, 2] = jnp.minimum(s, c - RB)
                items[k, 3] = s
                items[k, 4] = jnp.minimum(s + RB, z)
                return k + 1

            cnt = lax.fori_loop(0, (jnp.maximum(z - a, 0) + RB - 1) // RB, put, cnt)

    def copies(i, slot, op):
        g = items[i, 1]
        st = pl.multiple_of(items[i, 2], AL)
        for q, (pre, lo, hi, c) in enumerate(parts):
            @pl.when(items[i, 0] == q)
            def _():
                for k, dst in enumerate((xb, gb)):
                    src = arrs[2 * q + k]
                    view = src.at[g, pl.ds(st, RB)] if pre is None else src.at[g, pre[k], pl.ds(st, RB)]
                    op(pltpu.make_async_copy(view, dst.at[slot], sin.at[slot, k]))

    start = lambda cp: cp.start()
    wait = lambda cp: cp.wait()

    @pl.when(cnt > 0)
    def _():
        copies(0, 0, start)

    def step(i, carry):
        slot = lax.rem(i, 2)

        @pl.when(i + 1 < cnt)
        def _():
            copies(i + 1, 1 - slot, start)

        copies(i, slot, wait)
        row = items[i, 2] + lax.broadcasted_iota(I32, (RB, w), 0)
        keep = (row >= items[i, 3]) & (row < items[i, 4])
        x = jnp.where(keep, xb[slot].astype(F32), 0.0).astype(BF16)
        g = jnp.where(keep, gb[slot].astype(F32), 0.0).astype(BF16)
        h1f = jnp.dot(x, w1[0], preferred_element_type=F32).astype(BF16).astype(F32)
        h3f = jnp.dot(x, w3[0], preferred_element_type=F32).astype(BF16).astype(F32)
        da = _nt(g, w2[0]).astype(BF16).astype(F32)
        s = 0.5 * jnp.tanh(0.5 * h1f) + 0.5
        silu = h1f * s
        a = (silu * h3f).astype(BF16)
        dh1 = (da * h3f * (s + silu * (1.0 - s))).astype(BF16)
        dh3 = (da * silu).astype(BF16)
        dw1[0] += _tn(x, dh1)
        dw3[0] += _tn(x, dh3)
        dw2[0] += _tn(a, g)
        return carry

    lax.fori_loop(0, cnt, step, 0)


def _share(meta, arrs, parts, w1, w3, w2, prev, dims):
    ns, ne, el = dims
    ng = ns * el // ne
    w = w1.shape[1]
    fs = w1.shape[2] // ng
    di = ns * ne + 1
    cap = sum(ng * (c // RB + 2) for _, _, _, c in parts)
    in_specs = [ANY] * len(arrs) + [
        pl.BlockSpec((1, w, fs), lambda j, m: (j, 0, m[di])),
        pl.BlockSpec((1, w, fs), lambda j, m: (j, 0, m[di])),
        pl.BlockSpec((1, fs, w), lambda j, m: (j, m[di], 0))]
    acc = [pl.BlockSpec((1, w, fs), lambda j, m: (j, 0, 0)), pl.BlockSpec((1, w, fs), lambda j, m: (j, 0, 0)),
           pl.BlockSpec((1, fs, w), lambda j, m: (j, 0, 0))]
    first = prev is None
    args = (meta,) + tuple(arrs) + (w1, w3, w2) + (() if first else tuple(prev))
    na = len(arrs) + 4
    rows = ng * parts[0][3]
    return pl.pallas_call(
        functools.partial(_share_kernel, dims, parts, first),
        grid_spec=pltpu.PrefetchScalarGridSpec(
            num_scalar_prefetch=1, grid=(el,), in_specs=in_specs + ([] if first else acc), out_specs=acc,
            scratch_shapes=[pltpu.VMEM((2, RB, w), BF16), pltpu.VMEM((2, RB, w), BF16),
                            pltpu.SMEM((cap, 5), I32), pltpu.SemaphoreType.DMA((2, 2))]),
        out_shape=[jax.ShapeDtypeStruct((el, w, fs), F32), jax.ShapeDtypeStruct((el, w, fs), F32),
                   jax.ShapeDtypeStruct((el, fs, w), F32)],
        input_output_aliases={} if first else {na: 0, na + 1: 1, na + 2: 2},
        compiler_params=pltpu.CompilerParams(vmem_limit_bytes=VMEM_LIMIT),
        cost_estimate=pl.CostEstimate(flops=8 * rows * w * fs, bytes_accessed=4 * rows * w, transcendentals=0),
        name="share",
    )(*args)


def _take_kernel(tb, idx, d0, d1, o, buf, row):
    i = pl.program_id(0)
    n, w = d0.shape

    @pl.when(i == 0)
    def _():
        for k, s in enumerate((d0, d1)):
            def fill(b, c, k=k, s=s):
                buf[pl.ds(k * n + b * 64, 64), :] = s[pl.ds(b * 64, 64), :].astype(F32)
                return c

            lax.fori_loop(0, n // 64, fill, 0)
        buf[pl.ds(2 * n, 8), :] = jnp.zeros((8, w), F32)

    def step(t, c):
        for u in range(8):
            row[pl.ds(t * 8 + u, 1), :] = buf[pl.ds(idx[i * tb + t * 8 + u], 1), :]
        return c

    lax.fori_loop(0, tb // 8, step, 0)
    o[...] = row[...].astype(BF16)


def _take(idx, d0, d1, tb=512):
    n, w = d0.shape
    t = idx.shape[0]
    whole = pl.BlockSpec((n, w), lambda i, m: (0, 0), pipeline_mode=pl.Buffered(1))
    return pl.pallas_call(
        functools.partial(_take_kernel, tb),
        grid_spec=pltpu.PrefetchScalarGridSpec(
            num_scalar_prefetch=1, grid=(t // tb,), in_specs=[whole, whole],
            out_specs=pl.BlockSpec((tb, w), lambda i, m: (i, 0)),
            scratch_shapes=[pltpu.VMEM((2 * n + 8, w), F32), pltpu.VMEM((tb, w), F32)]),
        out_shape=jax.ShapeDtypeStruct((t, w), BF16),
        compiler_params=pltpu.CompilerParams(vmem_limit_bytes=48 * 1024 * 1024),
        cost_estimate=pl.CostEstimate(flops=20 * t * w, bytes_accessed=8 * n * w, transcendentals=0),
        name="take",
    )(idx, d0, d1)


def solution(mesh):
    np_ = mesh.shape['expert']
    nd = mesh.shape['data']
    tok = P(('data', 'expert'), None)
    buf = P(('data', 'expert'), None, None)
    wsp = P('expert', None, None)

    def body(dy, gates, topk_idx, slot, yd, xd, h1, h3, w1, w3, w2):
        _, d = dy.shape
        el = w1.shape[0]
        ne = np_ * el
        ns = nd * np_
        cap = xd.shape[1] // np_
        dims = (ns, ne, el)
        e = lax.axis_index('expert')
        dd = lax.axis_index('data')
        ex = topk_idx[:, 0]
        sl = slot[:, 0]
        alld = _extents(ex, sl, ne, (nd, np_))
        meta = jnp.concatenate([alld, e[None].astype(I32), dd[None].astype(I32)])
        rows = jnp.bitwise_and(alld + (AL - 1), -AL).reshape(nd, np_, np_, el).sum(axis=(1, 3))
        most = jnp.max(rows)
        pair = jnp.max(rows.sum(axis=1))
        theirs = rows[dd, 1 - e]
        rel = jnp.bitwise_xor(ex, e.astype(I32) * el)
        flat = jnp.where(sl >= 0, rel * cap + sl, ne * cap)

        swap = [(0, 1), (1, 0)]

        def gather(v):
            return lax.all_gather(v, 'data')

        def path(bounds, win, *args):
            return work(bounds, win, *args)

        def work(bounds, win, dy, gates, flat, yd, xd, h1, h3, w1, w3, w2, meta, theirs):
            half = bounds[-1]
            x2 = xd.reshape(el * np_ * cap, d)
            xl = _pack(meta, x2, x2, dims, bounds, win, True)
            xa = gather(xl[0])
            v = (gates * dy.astype(F32)).astype(BF16)
            slots, _ = lax.optimization_barrier((flat, xl[0]))
            send = jnp.zeros((ne * cap, d), BF16).at[slots].set(v, mode='drop').reshape(2, el, cap, d)
            g0 = send[0]
            g1 = lax.ppermute(send[1], 'expert', swap)
            gl = _pack(meta, g0.reshape(el * cap, d), g1.reshape(el * cap, d), dims, bounds, win, False)
            ga = gather(gl[0])
            if win:
                own_row = lax.broadcasted_iota(I32, (win, d), 0) < win - jnp.maximum(theirs - half, 0)
                top = jnp.stack([jnp.where(own_row, m[2], lax.ppermute(m[3], 'expert', swap)) for m in (xl, gl)])
                mid = jnp.stack([xl[1], gl[1]])
                ta = gather(top)
                ma = gather(mid)
                tb = lax.ppermute(ta, 'expert', swap)
            else:
                mid = jnp.stack([xl[1], gl[1]])
                ma = gather(mid)
            o0, o1 = _own(meta, g0, g1, h1, h3, w1, w3, w2, dims)
            b1 = lax.ppermute(o1, 'expert', swap)
            dx = _take(flat, o0.reshape(el * cap, d), b1.reshape(el * cap, d))
            dg = jnp.einsum('tkd,td->tk', yd, dy, preferred_element_type=F32)
            ws = (w1, w3, w2)
            acc = _share(meta, (xa, ga), [(None, 0, bounds[1], bounds[1])], *ws, None, dims)
            if win:
                acc = _share(meta, (ta, ta, tb, tb), [((0, 1), bounds[2], half, win), ((0, 1), half, None, win)], *ws, acc, dims)
            acc = _share(meta, (ma, ma), [((0, 1), bounds[1], bounds[2], bounds[2] - bounds[1])], *ws, acc, dims)
            return dx, dg, acc[0], acc[1], acc[2]

        win = 1024
        tiers = [(2816, win), (2944, win), (3136, win)]
        paths = [functools.partial(path, (0, n - w_ - 512, n - w_, n), w_) for n, w_ in tiers]
        full = np_ * cap * el
        paths.append(functools.partial(path, (0, full // 2, full), 0))
        pick = jnp.int32(0)
        for n, w_ in tiers:
            pick = pick + ((pair > 2 * n) | (most > n + w_)).astype(I32)
        return lax.switch(pick, paths, dy, gates, flat, yd, xd, h1, h3, w1, w3, w2, meta, theirs)

    return jax.shard_map(body, mesh=mesh,
                         in_specs=(tok, tok, tok, tok, buf, buf, buf, buf, wsp, wsp, wsp),
                         out_specs=(tok, tok, P('expert', None, 'data'), P('expert', None, 'data'), P('expert', 'data', None)),
                         check_vma=False)
```

time: 692 us -> 593 us (0.86)
  the two profiles are of different devices: /device:TPU:0 before, /device:TPU:1 now
where the time goes in v2:
time: 593 us; the launch traced here: 586 us
  Pallas kernels  347 us (59%)
  waiting for transfers between devices  149 us (25%)
  other arithmetic  40.4 us (7%)
  loops' own time  19.3 us (3%)
  between operations  17.9 us (3%)
  local copies, waits for them, and re-layouts  10.7 us (2%)
    pallas_call x3, Pallas kernels, _share(): pl.pallas_call(functools.partial(_share_kernel, dims, parts, first), grid...  186 us
    all_gather x4, waiting for transfers between devices, gather(): return lax.all_gather(v, 'data')  138 us
    pallas_call x1, Pallas kernels, _own(): pl.pallas_call(functools.partial(_own_kernel, dims, cap), grid_spec=pltpu...  112 us
    pallas_call x1, Pallas kernels, _take(): pl.pallas_call(functools.partial(_take_kernel, tb), grid_spec=pltpu.Prefe...  26.4 us
    scatter x1, other arithmetic, work(): jnp.zeros((ne * cap, d), BF16).at[slots].set(v, mode='drop')  25 us
    another operation x1, loops' own time, body(): lax.switch(pick, paths, dy, gates, flat, yd, xd, h1, h3, w1, w3, w2, meta...  19.3 us
    pallas_call x2, Pallas kernels, _pack(): pl.pallas_call(functools.partial(_pack_kernel, dims, bounds, win, base_e)...  14.7 us
  transfers between devices with their start and end apart: 9, of which 5 were waited for; matrix products, arithmetic and copies ran while one was open for 1% of the time, Pallas kernels for 49%

profile of v2, /device:TPU:1, one launch (start us, length us, event | category | flops | bytes accessed | tf_op | source)
XLA Modules:
  0.0 585.6 jit_solution(6188786610375609915)
XLA Ops:
  7.2 7.4 %extents.1 = s32[8,8,128]{2,1,0:T(8,128)} custom-call(s32[32,128]{1,0:T(8,128)} %bitcast.142, s32[32,128]{1,0:T(8,128)} %bitcast.143), custom_call_target="tpu_custom_call" | custom-call | bytes 65536 | tf_op jit(solution)/shard_map/extents/pallas_call | solution.py:138
  14.6 1.0 slice_reduce_fusion
  15.6 0.1 reshape_squeeze.11
  15.7 0.1 pad_add_fusion
  15.8 0.8 compare_select_fusion.4
  16.6 0.1 and.19
  16.6 0.1 reduce_sum.28
  16.8 0.6 reduce_max.19
  18.1 0.1 reduce_sum.26
  18.2 0.1 reduce_sum.27
  18.3 0.6 reduce_max.18
  22.2 556.0 %conditional.1 = (f32[4,768,768]{2,1,0:T(8,128)}, f32[4,768,768]{2,1,0:T(8,128)}, f32[4,768,768]{2,1,0:T(8,128)}, bf16[4096,768]{1,0:T(8,128)(2,1)}, f32[4096,1]{0,1:T(1,128)S(1)}) conditional(s32[]{:T(128)} %clamp.3, (bf16[4,1280,768]{2,1,0:T(8,128)(2,1)}, s32[66]{0:T(128)S(1)}, s32[4096]{0:T(1024)S(1)}, ...), branch_computations={%region_5.7_spmd, %region_7.0_spmd, %region_9.0_spmd, %region_11.0... | conditional | flops 169203220480 | bytes 649724352 | solution.py:500
  29.1 0.0 all-gather.41.cloned.1.call-start
  29.2 0.0 copy-start.33
  29.2 5.4 pack.10
  34.6 0.0 copy-start.18
  34.6 0.9 copy-done.18
  35.5 0.0 copy-done.33
  35.5 25.0 %scatter_custom_fusion.1 = bf16[5120,768]{1,0:T(8,128)(2,1)} fusion(s32[4096]{0:T(1024)S(1)} %compare_select_fusion.1, bf16[4096,768]{1,0:T(8,128)(2,1)} %get-tuple-element.132, f32[4096]{0:T(1024)S(1)} %bitcast.139, bf16[]{:T(256)} %constant.32.clone), kind=kCustom, calls=%fused_computation.21 | custom fusion | flops 9437184 | bytes 14172162 | tf_op jit(solution)/shard_map/cond/branch_1_fun/scatter | solution.py:466
  60.5 3.6 fusion.27
  64.1 0.0 collective-permute-start.5
  64.2 0.5 collective-permute-start.7
  64.7 6.3 %collective-permute-done.5.g1 = bf16[4,640,768]{2,1,0:T(8,128)(2,1)S(1)} collective-permute-done((bf16[4,640,768]{2,1,0:T(8,128)(2,1)S(1)}, bf16[4,640,768]{2,1,0:T(8,128)(2,1)S(1)}, u32[]{:S(2)}, u32[]{:S(2)}) %collective-permute-start.5) | collective-permute-done | bytes 3932192 | tf_op jit(solution)/shard_map/cond/branch_1_fun/ppermute | solution.py:468
  71.0 9.3 %pack.11 = (bf16[1408,768]{1,0:T(8,128)(2,1)}, bf16[512,768]{1,0:T(8,128)(2,1)S(1)}, bf16[1024,768]{1,0:T(8,128)(2,1)S(1)}, bf16[1024,768]{1,0:T(8,128)(2,1)}) custom-call(s32[66]{0:T(128)S(1)} %get-tuple-element.127.meta, bf16[2560,768]{1,0:T(8,128)(2,1)S(1)} %get-tuple-element.431.src0, bf16[2560,768]{1,0:T(8,128)(2,1)S(1)} %bitcast.88), custom_call_target="tpu_custom_call" | custom-call | bytes 12189696 | tf_op jit(solution)/shard_map/cond/branch_1_fun/pack/pallas_call | solution.py:89
  80.2 0.0 copy-done.5
  80.3 0.0 copy-start.1
  80.3 1.9 copy-done.1
  82.2 0.9 copy-done.24
  83.1 0.0 collective-permute-start.8
  83.1 0.1 copy.51
  83.2 0.6 dynamic_slice.5
  84.3 0.0 collective-permute-done.7
  84.3 2.5 collective-permute-done.8
  86.8 2.3 select_bitcast_fusion.3
  89.1 0.0 copy-start.19
  89.1 0.0 copy-start.25
  89.1 1.9 pad_maximum_fusion.2
  91.0 0.0 all-gather.41.cloned.1.call-update
  91.1 0.0 all-gather.43.cloned.1.call-start
  91.1 0.7 all-gather.43.cloned.1.call-update
  91.8 0.0 all-gather.45.cloned.1.call-start
  91.9 0.7 all-gather.45.cloned.1.call-update
  92.6 0.0 all-gather.39.cloned.1.call-start
  92.6 0.0 copy-done.19
  92.6 0.0 copy-done.25
  92.6 1.3 pad_maximum_fusion.3
  93.9 0.0 all-gather.39.cloned.1.call-update
  93.9 114.5 %all-gather.41.cloned.1.call-done = bf16[8,1024,768]{2,1,0:T(8,128)(2,1)} async-done(((bf16[2,1024,768]{2,1,0:T(8,128)(2,1)}), bf16[8,1024,768]{2,1,0:T(8,128)(2,1)}) %all-gather.41.cloned.1.call-update) | async-done | bytes 12582928 | tf_op jit(solution)/shard_map/cond/branch_1_fun/all_gather | solution.py:454
  208.4 0.8 collective-permute-start.9
  209.2 112.2 %own.5 = (bf16[4,640,768]{2,1,0:T(8,128)(2,1)}, bf16[4,640,768]{2,1,0:T(8,128)(2,1)}) custom-call(s32[66]{0:T(128)S(1)} %get-tuple-element.127.meta, bf16[4,640,768]{2,1,0:T(8,128)(2,1)} %bitcast.84, bf16[4,640,768]{2,1,0:T(8,128)(2,1)} %copy-done.5, bf16[4,1280,3072]{2,1,0:T(8,128)(2,1)} %get-tuple-element.133.h1, ...), custom_call_target="tpu_custom_call" | custom-call | flops 72477573120 | bytes 88080384 | tf_op jit(solution)/shard_map/cond/branch_1_fun/own/pallas_call | solution.py:248
  321.4 0.0 collective-permute-start.6
  321.5 0.0 copy-start.13
  321.5 6.5 %fusion.7 = f32[4096]{0:T(1024)S(1)} fusion(bf16[4096,768]{1,0:T(8,128)(2,1)} %get-tuple-element.132, bf16[4096,1,768]{2,0,1:T(8,128)(2,1)} %get-tuple-element.140), kind=kLoop, calls=%fused_computation.20 | loop fusion | flops 12578816 | bytes 12599296 | tf_op jit(solution)/shard_map/cond/branch_1_fun/tkd,td->tk/dot_general | solution.py:484
  327.9 0.5 collective-permute-done.6
  328.4 1.9 copy-done.29
  330.4 26.4 %take.5 = bf16[4096,768]{1,0:T(8,128)(2,1)} custom-call(s32[4096]{0:T(1024)S(1)} %get-tuple-element.130.idx, bf16[2560,768]{1,0:T(8,128)(2,1)S(1)} %bitcast.94, bf16[2560,768]{1,0:T(8,128)(2,1)} %bitcast.130), custom_call_target="tpu_custom_call" | custom-call | flops 62914560 | bytes 15728640 | tf_op jit(solution)/shard_map/cond/branch_1_fun/take/pallas_call | solution.py:411
  356.8 23.4 %all-gather.45.cloned.1.call-done = bf16[5632,768]{1,0:T(8,128)(2,1)} async-done(((bf16[1408,768]{1,0:T(8,128)(2,1)}), bf16[5632,768]{1,0:T(8,128)(2,1)}) %all-gather.45.cloned.1.call-update) | async-done | bytes 8650768 | tf_op jit(solution)/shard_map/cond/branch_1_fun/all_gather | solution.py:454
  380.2 78.0 %share.14 = (f32[4,768,768]{2,1,0:T(8,128)}, f32[4,768,768]{2,1,0:T(8,128)}, f32[4,768,768]{2,1,0:T(8,128)}) custom-call(s32[66]{0:T(128)S(1)} %get-tuple-element.127.meta, bf16[4,1408,768]{2,1,0:T(8,128)(2,1)} %bitcast.154, bf16[4,1408,768]{2,1,0:T(8,128)(2,1)} %bitcast.155, bf16[4,768,3072]{2,1,0:T(8,128)(2,1)} %get-tuple-element.135.w1.rest_2_.rest_4_, ...), custom_call_target="tpu_custom_call" | custom-call | flops 26575110144 | bytes 17301504 | tf_op jit(solution)/shard_map/cond/branch_1_fun/share/pallas_call | solution.py:369
  458.2 0.0 collective-permute-done.9.rest_2_.rest_3_
  458.3 62.1 %share.15 = (f32[4,768,768]{2,1,0:T(8,128)}, f32[4,768,768]{2,1,0:T(8,128)}, f32[4,768,768]{2,1,0:T(8,128)}) custom-call(s32[66]{0:T(128)S(1)} %get-tuple-element.127.meta, bf16[4,2,1024,768]{3,2,1,0:T(8,128)(2,1)} %bitcast.115, bf16[4,2,1024,768]{3,2,1,0:T(8,128)(2,1)} %bitcast.116, ...), custom_call_target="tpu_custom_call", output_to_operand_aliasing={{0}: (8, {}), {1}: (9, {}), {2}: (10, {})} | custom-call | flops 19327352832 | bytes 12582912 | tf_op jit(solution)/shard_map/cond/branch_1_fun/share/pallas_call | solution.py:369
  520.3 0.0 all-gather.39.cloned.1.call-done
  520.3 46.4 %share.16 = (f32[4,768,768]{2,1,0:T(8,128)}, f32[4,768,768]{2,1,0:T(8,128)}, f32[4,768,768]{2,1,0:T(8,128)}) custom-call(s32[66]{0:T(128)S(1)} %get-tuple-element.127.meta, bf16[4,2,512,768]{3,2,1,0:T(8,128)(2,1)} %bitcast.122, bf16[4,2,512,768]{3,2,1,0:T(8,128)(2,1)} %bitcast.123, ...), custom_call_target="tpu_custom_call", output_to_operand_aliasing={{0}: (6, {}), {1}: (7, {}), {2}: (8, {})} | custom-call | flops 9663676416 | bytes 6291456 | tf_op jit(solution)/shard_map/cond/branch_1_fun/share/pallas_call | solution.py:369
  578.2 0.0 copy-start.36
  578.2 0.6 copy-done.36
  (7 shorter events, 0.0 us)
Async XLA Ops:
  29.1 179.3 %all-gather.41.cloned.1.call-start = ((), (), s32[]{:S(2)}) async-start(), calls=%async_computation.5 | async-start | bytes 15728640 | tf_op jit(solution)/shard_map/cond/branch_1_fun/all_gather | solution.py:454
  29.2 6.3 %copy-start.33 = (f32[4096,1]{0,1:T(1,128)S(1)}, f32[4096,1]{0,1:T(1,128)}, u32[]{:S(2)}) copy-start(f32[4096,1]{0,1:T(1,128)} %get-tuple-element.131) | copy-start | bytes 49156 | tf_op jit(solution)/shard_map/cond
  34.6 0.9 copy-start.18
  64.1 6.8 %collective-permute-start.5 = (bf16[4,640,768]{2,1,0:T(8,128)(2,1)S(1)}, bf16[4,640,768]{2,1,0:T(8,128)(2,1)S(1)}, u32[]{:S(2)}, u32[]{:S(2)}) collective-permute-start(bf16[4,640,768]{2,1,0:T(8,128)(2,1)S(1)} %bitcast.127), channel_id=1, source_target_pairs={{0,1},{1,0},{2,3},{3,2},{4,5},{5,4},{6,7},{7,6}} | collective-permute-start | bytes 11796488 | tf_op jit(solution)/shard_map/cond/branch_1_fun/ppermute | solution.py:468
  64.2 20.1 %collective-permute-start.7 = (bf16[1024,768]{1,0:T(8,128)(2,1)}, bf16[1024,768]{1,0:T(8,128)(2,1)}, u32[]{:S(2)}, u32[]{:S(2)}) collective-permute-start(bf16[1024,768]{1,0:T(8,128)(2,1)} %get-tuple-element.145), channel_id=1, source_target_pairs={{0,1},{1,0},{2,3},{3,2},{4,5},{5,4},{6,7},{7,6}} | collective-permute-start | bytes 4718600 | tf_op jit(solution)/shard_map/cond/branch_1_fun/ppermute | solution.py:473
  70.9 9.3 %copy-start.5 = (bf16[4,640,768]{2,1,0:T(8,128)(2,1)}, bf16[4,640,768]{2,1,0:T(8,128)(2,1)S(1)}, u32[]{:S(2)}) copy-start(bf16[4,640,768]{2,1,0:T(8,128)(2,1)S(1)} %collective-permute-done.5.g1) | copy-start | bytes 11796484 | tf_op jit(solution)/shard_map/cond
  80.3 1.9 copy-start.1
  82.2 0.9 copy-start.24
  83.1 3.8 collective-permute-start.8
  89.1 3.5 copy-start.19
  89.1 3.5 copy-start.25
  91.1 265.7 %all-gather.43.cloned.1.call-start = ((), (), s32[]{:S(2)}) async-start(), calls=%async_computation.6 | async-start | bytes 10813440 | tf_op jit(solution)/shard_map/cond/branch_1_fun/all_gather | solution.py:454
  91.8 288.4 %all-gather.45.cloned.1.call-start = ((), (), s32[]{:S(2)}) async-start(), calls=%async_computation.7 | async-start | bytes 10813440 | tf_op jit(solution)/shard_map/cond/branch_1_fun/all_gather | solution.py:454
  92.6 427.8 %all-gather.39.cloned.1.call-start = ((), (), s32[]{:S(2)}) async-start(), calls=%async_computation.4 | async-start | bytes 7864320 | tf_op jit(solution)/shard_map/cond/branch_1_fun/all_gather | solution.py:454
  208.4 249.8 %collective-permute-start.9 = (bf16[4,2,1024,768]{3,2,1,0:T(8,128)(2,1)}, bf16[4,2,1024,768]{3,2,1,0:T(8,128)(2,1)}, u32[]{:S(2)}, u32[]{:S(2)}) collective-permute-start(bf16[4,2,1024,768]{3,2,1,0:T(8,128)(2,1)} %bitcast.114), channel_id=1, source_target_pairs={{0,1},{1,0},{2,3},{3,2},{4,5},{5,4},{6,7},{7,6}} | collective-permute-start | bytes 37748744 | tf_op jit(solution)/shard_map/cond/branch_1_fun/ppermute | solution.py:477
  321.4 7.0 %collective-permute-start.6 = (bf16[4,640,768]{2,1,0:T(8,128)(2,1)}, bf16[4,640,768]{2,1,0:T(8,128)(2,1)S(1)}, u32[]{:S(2)}, u32[]{:S(2)}) collective-permute-start(bf16[4,640,768]{2,1,0:T(8,128)(2,1)} %get-tuple-element.139), channel_id=1, source_target_pairs={{0,1},{1,0},{2,3},{3,2},{4,5},{5,4},{6,7},{7,6}} | collective-permute-start | bytes 11796488 | tf_op jit(solution)/shard_map/cond/branch_1_fun/ppermute | solution.py:482
  321.5 8.9 %copy-start.13 = (bf16[4,640,768]{2,1,0:T(8,128)(2,1)S(1)}, bf16[4,640,768]{2,1,0:T(8,128)(2,1)}, u32[]{:S(2)}) copy-start(bf16[4,640,768]{2,1,0:T(8,128)(2,1)} %get-tuple-element.138) | copy-start | bytes 11796484 | tf_op jit(solution)/shard_map/cond
  328.4 1.9 copy-start.29
  578.2 0.6 copy-start.36
Sparse Core Ops, SparseCore 0:
  91.2 117.1 all-gather.40
  210.2 84.0 all-gather.42
  296.1 84.0 all-gather.44
  381.8 64.4 all-gather.38
